TPU v7x, 32 devices: a whole 2x2x4 slice. The times are simulated.
32 devices in a mesh: batch: 2 (over core), token: 8 (over z, x), hidden: 2 (over y).
Axes of the slice: x: 2, y: 2, z: 4, core: 2. Of those that a mesh axis runs over, the one named last changes fastest.
Arguments:
- hist_len: int32 [128], replicated, may hold values from 32 to 512, as said below
- queries: bfloat16 [32, 1536], P(None, 'token'), may hold values from -4 to 4
- history_keys: bfloat16 [384, 1536, 128], P(('batch', 'hidden'), 'token'), may hold values from -192 to 192
- cached_history_values: bfloat16 [384, 1536, 128], P(('batch', 'hidden'), 'token'), may hold values from -6 to 6
- gain_mix: float32 [1536], replicated, may hold values from 0.25 to 1.75
- w_up: bfloat16 [32, 1536, 3072], P('token', None, 'hidden'), may hold values from -0.15625 to 0.15625
- w_down: bfloat16 [32, 3072, 1536], P('token', 'hidden'), may hold values from -0.109375 to 0.109375
- gain_out: float32 [1536], replicated, may hold values from 0.25 to 1.75
Outputs:
- mixer_out: bfloat16 [128, 32, 1536], P(('batch', 'hidden'), 'token')
Inputs may be any that keep to these rules, and one draw needn't show every extreme that they name: `hist_len`: along batch+hidden, the requests of each index need between 32 and 96 slots, indices 2i and 2i + 1 need 4 * 32 slots together, and some index needs exactly 96; within an index, requests 2j and 2j + 1 need from 2 to 6 slots together.
All inputs are finite; a program needn't handle non-finite values.
Results may differ from a plain program's by a relative error of at most 0.015.
Values may be sent and summed in bfloat16 or wider, within the bound.
No kernel may reach another device: no remote copies, remote signals or barrier semaphores. Data moves between devices by JAX's collectives and lax.ppermute only.
A program may use at most 128 MiB of HBM per device.

v0:
```python
import jax
import jax.numpy as jnp
from jax import lax
from jax.sharding import PartitionSpec as P

TOKEN_COUNT = 32
MODEL_WIDTH = 1536
BLOCK_POSITIONS = 128
REQ_DEV = 32
EPSILON = 1e-05
NEGATIVE_FILL = -1e30


def slot_layout(lengths, slot_count, block_rows):
    request_count = lengths.shape[0]
    blocks = (lengths + block_rows - 1) // block_rows
    block_ends = jnp.cumsum(blocks)
    block_starts = block_ends - blocks
    slot_index = jnp.arange(slot_count, dtype=jnp.int32)
    owners = jnp.sum((block_ends[None, :] <= slot_index[:, None]).astype(jnp.int32), axis=1)
    onehot = owners[:, None] == jnp.arange(request_count, dtype=jnp.int32)[None, :]
    start_of = jnp.sum(jnp.where(onehot, block_starts[None, :], 0), axis=1)
    length_of = jnp.sum(jnp.where(onehot, lengths[None, :], 0), axis=1)
    valid_rows = jnp.clip(length_of - (slot_index - start_of) * block_rows, 0, block_rows)
    return (onehot, valid_rows)


def block_partials(query_heads, slot_keys, slot_values, valid_rows, score_scale):
    scores = (
        jnp.einsum("qhs,nhsp->nqhp", query_heads, slot_keys, preferred_element_type=jnp.float32)
        * score_scale
    )
    position = jnp.arange(slot_keys.shape[-1], dtype=jnp.int32)
    in_range = position[None, None, None, :] < valid_rows[:, None, None, None]
    scores = jnp.where(in_range, scores, NEGATIVE_FILL)
    maxima = jnp.max(scores, axis=-1)
    softmax_terms = jnp.where(in_range, jnp.exp(scores - maxima[..., None]), 0.0)
    totals = jnp.sum(softmax_terms, axis=-1)
    weighted = jnp.einsum(
        "nqhp,nhsp->nqhs",
        softmax_terms.astype(jnp.bfloat16),
        slot_values,
        preferred_element_type=jnp.float32,
    )
    return (maxima, totals, weighted)


def combine_blocks(maxima, totals, weighted, onehot):
    owned = onehot.astype(jnp.float32)
    is_live = jnp.sum(owned, axis=1) > 0.5
    masked_max = jnp.where(onehot[:, :, None, None], maxima[:, None, :, :], NEGATIVE_FILL)
    request_max = jnp.max(masked_max, axis=0)
    owner_max = jnp.einsum("nr,rqh->nqh", owned, request_max, precision=lax.Precision.HIGHEST)
    factor = jnp.exp(jnp.where(is_live[:, None, None], maxima - owner_max, NEGATIVE_FILL))
    denominator = jnp.einsum("nr,nqh->rqh", owned, factor * totals, precision=lax.Precision.HIGHEST)
    numerator = jnp.einsum(
        "nr,nqhs->rqhs", owned, factor[..., None] * weighted, precision=lax.Precision.HIGHEST
    )
    return (numerator / denominator[..., None]).astype(jnp.bfloat16)


def layer_norm(summand):
    average = jnp.mean(summand, axis=-1, keepdims=True)
    centred = summand - average
    variance = jnp.mean(centred * centred, axis=-1, keepdims=True)
    return centred * lax.rsqrt(variance + EPSILON)


def local(hist_len, queries, history_keys, cached_history_values, gain_mix, w_up, w_down, gain_out):
    group_size = lax.axis_size(("batch", "hidden"))
    my_index = lax.axis_index(("batch", "hidden"))
    head_size = MODEL_WIDTH // TOKEN_COUNT
    local_heads = history_keys.shape[1] // head_size
    slot_count = history_keys.shape[0]
    score_scale = head_size ** (-0.5)
    query_heads = queries.reshape(TOKEN_COUNT, local_heads, head_size)
    all_lengths = hist_len.reshape(group_size, REQ_DEV)
    peer_ids = jnp.arange(group_size, dtype=jnp.int32)
    mine_hot = peer_ids == my_index
    own_lengths = jnp.sum(jnp.where(mine_hot[:, None], all_lengths, 0), axis=0)
    onehot, valid_rows = slot_layout(own_lengths, slot_count, BLOCK_POSITIONS)
    slot_keys = history_keys.reshape(slot_count, local_heads, head_size, BLOCK_POSITIONS)
    slot_values = cached_history_values.reshape(slot_count, local_heads, head_size, BLOCK_POSITIONS)
    maxima, totals, weighted = block_partials(
        query_heads, slot_keys, slot_values, valid_rows, score_scale
    )
    attended = combine_blocks(maxima, totals, weighted, onehot)
    unmixed = lax.all_to_all(
        attended.reshape(REQ_DEV, TOKEN_COUNT, local_heads * head_size),
        "token",
        split_axis=1,
        concat_axis=2,
        tiled=True,
    )
    mixed_rows = jnp.transpose(attended, (0, 2, 1, 3)).reshape(
        REQ_DEV, local_heads, TOKEN_COUNT * head_size
    )
    joined = mixed_rows.astype(jnp.float32) + unmixed.astype(jnp.float32)
    normed = (layer_norm(joined) * gain_mix).astype(jnp.bfloat16)
    lifted = jnp.einsum(
        "ntd,tdf->ntf",
        lax.all_gather(normed, "hidden", axis=0, tiled=True),
        w_up,
        preferred_element_type=jnp.float32,
    )
    activated = jax.nn.gelu(lifted, approximate=False).astype(jnp.bfloat16)
    partial_sums = jnp.einsum("ntf,tfd->ntd", activated, w_down, preferred_element_type=jnp.float32)
    summed = lax.psum_scatter(partial_sums, "hidden", scatter_dimension=0, tiled=True)
    return (layer_norm(summed + normed.astype(jnp.float32)) * gain_out).astype(jnp.bfloat16)


def solution(mesh):
    return jax.shard_map(
        local,
        mesh=mesh,
        in_specs=(
            P(),
            P(None, "token"),
            P(("batch", "hidden"), "token", None),
            P(("batch", "hidden"), "token", None),
            P(),
            P("token", None, "hidden"),
            P("token", "hidden", None),
            P(),
        ),
        out_specs=P(("batch", "hidden"), "token", None),
        check_vma=False,
    )
```

profile of v0, /device:TPU:0, one launch (start us, length us, event | category | flops | bytes accessed | tf_op | source)
XLA Modules:
  0.0 143.5 jit_solution(5583828405777841937)
XLA Ops:
  6.5 0.7 reshape.210
  7.9 0.5 broadcast_compare_fusion
  8.5 0.8 reshape.213
  9.3 6.7 %bitcast_reduce_fusion = (f32[96,32,4]{1,0,2:T(8,128)S(1)}, f32[4,96,128,32]{2,3,1,0:T(8,128)}) fusion(pred[96,128]{1,0:T(8,128)(4,1)S(1)} %iota_compare_fusion, bf16[96,4,48,128]{3,2,1,0:T(8,128)(2,1)} %bitcast.131, bf16[32,4,48,1]{2,1,0,3:T(4,128)(2,1)S(1)} %bitcast.134), kind=kOutput, calls=%fused_computation.2 | convolution fusion | flops 155701248 | bytes 11083776 | tf_op jit(solution)/shard_map/qhs,nhsp->nqhp/dot_general | solution.py:30
  16.1 0.7 copy.59
  16.8 6.0 %fusion.6 = (f32[96,32,4]{1,0,2:T(8,128)S(1)}, bf16[96,32,4,128]{3,1,0,2:T(8,128)(2,1)S(1)}) fusion(f32[4,96,128,32]{2,3,1,0:T(8,128)} %get-tuple-element.12, f32[96,32,4]{1,0,2:T(8,128)S(1)} %get-tuple-element.11, pred[96,128]{1,0:T(8,128)(4,1)S(1)} %iota_compare_fusion), kind=kLoop, calls=%fused_computation.10 | loop fusion | flops 9424896 | bytes 9547776 | tf_op jit(solution)/shard_map/reduce_sum | solution.py:38
  22.8 0.7 copy.63
  23.5 1.5 %select_reduce_fusion = f32[32,32,4]{1,2,0:T(4,128)S(1)} fusion(f32[96,32,4]{0,1,2:T(8,128)} %copy.59, pred[96,32]{0,1:T(8,128)(4,1)S(1)} %iota_compare_fusion.1), kind=kLoop, calls=%fused_computation.21 | loop fusion | flops 782336 | bytes 68608 | tf_op jit(solution)/shard_map/reduce_max | solution.py:52
  25.0 1.1 fusion.32
  26.2 1.1 fusion.68
  27.4 4.8 %bitcast_multiply_fusion = f32[96,32,4,48]{3,1,2,0:T(8,128)S(1)} fusion(f32[96,32,4]{1,2,0:T(4,128)S(1)} %copy.60, bf16[96,4,48,128]{3,2,1,0:T(8,128)(2,1)} %bitcast.130, bf16[96,32,4,128]{3,1,0,2:T(8,128)(2,1)S(1)} %get-tuple-element.10), kind=kOutput, calls=%fused_computation | convolution fusion | flops 151584768 | bytes 10272768 | tf_op jit(solution)/shard_map/nqhp,nhsp->nqhs/dot_general | solution.py:39
  32.3 8.8 %divide_convert_fusion = (bf16[32,32,4,48]{3,0,2,1:T(8,128)(2,1)S(1)}, f32[32,32,4,48]{3,0,2,1:T(8,128)}) fusion(f32[32,32,4]{0,2,1:T(4,128)S(1)} %copy.66, f32[96,32,4,48]{3,1,2,0:T(8,128)S(1)} %bitcast_multiply_fusion, s32[96]{0:T(128)S(1)} %copy-done.3), kind=kOutput, calls=%fused_computation.20 | convolution fusion | flops 226888704 | bytes 3555712 | tf_op jit(solution)/shard_map/nr,nqhs->rqhs/dot_general | solution.py:56
  41.1 0.5 copy.77
  41.7 1.4 reshape.224
  43.0 7.3 %all-to-all-start = ((bf16[32,32,192]{2,0,1:T(8,128)(2,1)}), bf16[32,32,192]{2,0,1:T(8,128)(2,1)S(1)}, u32[]{:S(2)}, u32[]{:S(2)}) async-start(bf16[32,32,192]{2,0,1:T(8,128)(2,1)} %reshape.224), calls=%async_computation | async-start | bytes 1048576 | tf_op jit(solution)/shard_map/all_to_all | solution.py:88
  50.3 0.2 reduce-scatter.2.cloned.1.call-start
  50.6 14.2 %all-to-all-done = bf16[32,32,192]{2,0,1:T(8,128)(2,1)S(1)} async-done(((bf16[32,32,192]{2,0,1:T(8,128)(2,1)}), bf16[32,32,192]{2,0,1:T(8,128)(2,1)S(1)}, u32[]{:S(2)}, u32[]{:S(2)}) %all-to-all-start) | async-done | bytes 393248 | tf_op jit(solution)/shard_map/all_to_all | solution.py:88
  64.9 0.6 copy.70
  65.6 0.6 copy.69
  66.2 1.3 reshape.217
  67.4 0.5 reshape.218
  67.9 3.9 %fusion.34 = (f32[32,4]{0,1:T(4,128)S(1)}, f32[32,4,32,48]{3,0,1,2:T(8,128)S(1)}) fusion(f32[32,4,32,48]{3,2,1,0:T(8,128)S(1)} %reshape.218, f32[32,4,32]{0,1,2:T(4,128)S(1)} %copy.64, f32[32,32,4,48]{3,0,2,1:T(8,128)} %get-tuple-element.14), kind=kLoop, calls=%fused_computation.50 | loop fusion | flops 982912 | bytes 2376192 | tf_op jit(solution)/shard_map/reduce_sum | solution.py:63
  71.8 2.6 %copy.65 = f32[32,4,32,48]{3,2,0,1:T(8,128)} copy(f32[32,4,32,48]{3,0,1,2:T(8,128)S(1)} %get-tuple-element.8) | data formatting | bytes 1572864 | tf_op jit(solution)/shard_map/convert_element_type | solution.py:98
  74.4 1.4 multiply_reduce_fusion
  75.8 2.9 %reshape.216 = f32[32,4,1536]{2,0,1:T(8,128)S(1)} reshape(f32[32,4,32,48]{3,2,0,1:T(8,128)} %copy.65) | data formatting | bytes 1572864 | tf_op jit(solution)/shard_map/convert_element_type | solution.py:98
  78.8 0.2 multiply_convert_fusion.1
  79.0 10.4 %all_gather.3 = bf16[64,4,1536]{2,0,1:T(8,128)(2,1)S(1)} all-gather(bf16[32,4,1536]{2,0,1:T(8,128)(2,1)S(1)} %multiply_convert_fusion.1), channel_id=1, replica_groups=mesh['batch'=2,'token'=8,'hidden'=2] {'hidden'}, dimensions={0}, use_global_device_ids=true | all-gather | bytes 1179648 | tf_op jit(solution)/shard_map/all_gather | solution.py:102
  89.4 17.5 %convolution_bitcast_fusion = f32[64,4,1536]{2,0,1:T(8,128)} fusion(bf16[4,1536,1536]{2,1,0:T(8,128)(2,1)} %param.14, bf16[64,4,1536]{2,0,1:T(8,128)(2,1)S(1)} %all_gather.3, bf16[4,1536,1536]{2,1,0:T(8,128)(2,1)} %param.13), kind=kOutput, calls=%fused_computation.14 | convolution fusion | flops 2441478144 | bytes 40108032 | tf_op jit(solution)/shard_map/ntf,tfd->ntd/dot_general | solution.py:107
  106.9 26.9 %reduce-scatter.2.cloned.1.call-done = f32[32,4,1536]{2,0,1:T(8,128)} async-done(((f32[64,4,1536]{2,0,1:T(8,128)}), f32[32,4,1536]{2,0,1:T(8,128)}) %reduce-scatter.2.cloned.1.call-update) | async-done | bytes 786448 | tf_op jit(solution)/shard_map/reduce_scatter | solution.py:108
  133.8 1.4 fusion.66
  135.2 0.2 multiply_reduce_fusion.1
  135.6 1.1 copy.72
  (35 shorter events, 1.3 us)
Async XLA Ops:
  7.7 0.7 copy-start.2
  27.4 4.9 %copy-start.3 = (s32[96]{0:T(128)S(1)}, s32[96]{0:T(128)}, u32[]{:S(2)}) copy-start(s32[96]{0:T(128)} %copy-done.2) | copy-start | bytes 1156
  43.0 21.8 %all-to-all-start = ((bf16[32,32,192]{2,0,1:T(8,128)(2,1)}), bf16[32,32,192]{2,0,1:T(8,128)(2,1)S(1)}, u32[]{:S(2)}, u32[]{:S(2)}) async-start(bf16[32,32,192]{2,0,1:T(8,128)(2,1)} %reshape.224), calls=%async_computation | async-start | bytes 1048576 | tf_op jit(solution)/shard_map/all_to_all | solution.py:88
  50.3 83.5 %reduce-scatter.2.cloned.1.call-start = ((), (), s32[]{:S(2)}) async-start(), calls=%async_computation.2 | async-start | bytes 2359296 | tf_op jit(solution)/shard_map/reduce_scatter | solution.py:108
  75.8 2.9 %copy-start.1 = (f32[32,4,1536]{2,0,1:T(8,128)S(1)}, f32[32,4,1536]{2,0,1:T(8,128)}, u32[]{:S(2)}) copy-start(f32[32,4,1536]{2,0,1:T(8,128)} %reshape.217) | copy-start | bytes 2359300
  75.8 2.9 %copy-start.4 = (f32[1536]{0:T(1024)S(1)}, f32[1536]{0:T(1024)}, u32[]{:S(2)}) copy-start(f32[1536]{0:T(1024)} %param.12) | copy-start | bytes 18436
  106.9 28.5 %copy-start.5 = (f32[1536]{0:T(1024)S(1)}, f32[1536]{0:T(1024)}, u32[]{:S(2)}) copy-start(f32[1536]{0:T(1024)} %param.15) | copy-start | bytes 18436
  133.8 1.4 copy-start
Sparse Core Ops, SparseCore 0:
  107.0 26.7 reduce-scatter.1
where the time goes:
time: 144 us
  waiting for transfers between devices  41.1 us (29%)
  matrix products  40.1 us (28%)
  other arithmetic  16 us (11%)
  local copies, waits for them, and re-layouts  14.9 us (10%)
  between operations  13.6 us (9%)
  blocking collectives  10.4 us (7%)
  starting transfers between devices  7.5 us (5%)
    reduce_scatter x1, waiting for transfers between devices, local(): lax.psum_scatter(partial_sums, 'hidden', scatter_dimension=0, tiled=True)  26.9 us
    dot_general x1, matrix products, local(): jnp.einsum('ntf,tfd->ntd', activated, w_down, preferred_element_type=jnp....  17.5 us
    all_to_all x1, waiting for transfers between devices, local(): lax.all_to_all(attended.reshape(REQ_DEV, TOKEN_COUNT, local_heads * head_...  14.2 us
    all_gather x1, blocking collectives, local(): lax.all_gather(normed, 'hidden', axis=0, tiled=True)  10.4 us
    dot_general x1, matrix products, combine_blocks(): jnp.einsum('nr,nqhs->rqhs', owned, factor[..., None] * weighted, precisio...  8.84 us
    convert_element_type x6, local copies, waits for them, and re-layouts, local(): joined = mixed_rows.astype(jnp.float32) + unmixed.astype(jnp.float32)  8.46 us
    all_to_all x1, starting transfers between devices, local(): lax.all_to_all(attended.reshape(REQ_DEV, TOKEN_COUNT, local_heads * head_...  7.28 us
    dot_general x1, matrix products, block_partials(): jnp.einsum('qhs,nhsp->nqhp', query_heads, slot_keys, preferred_element_ty...  6.72 us
  transfers between devices with their start and end apart: 2, of which 2 were waited for; matrix products, arithmetic and copies ran while one was open for 0% of the time, Pallas kernels for 0%

commit v1 on v0

--- a/solution.py
+++ b/solution.py
@@ -85,13 +85,14 @@
         query_heads, slot_keys, slot_values, valid_rows, score_scale
     )
     attended = combine_blocks(maxima, totals, weighted, onehot)
-    unmixed = lax.all_to_all(
-        attended.reshape(REQ_DEV, TOKEN_COUNT, local_heads * head_size),
-        "token",
-        split_axis=1,
-        concat_axis=2,
-        tiled=True,
-    )
+
+    def track_blocks(packet, out_dim, k_dim=2):
+        a_next = jnp.stack(jnp.split(packet, jax.lax.axis_size("token"), out_dim), 0)
+        return jnp.concatenate(
+            jax.lax.all_to_all(a_next, concat_axis=0, split_axis=0, axis_name="token"), k_dim
+        )
+
+    unmixed = track_blocks(attended.reshape(REQ_DEV, TOKEN_COUNT, local_heads * head_size), 1)
     mixed_rows = jnp.transpose(attended, (0, 2, 1, 3)).reshape(
         REQ_DEV, local_heads, TOKEN_COUNT * head_size
     )

time: 144 us -> 149 us (1.035)
  local copies, waits for them, and re-layouts: 14.9 us -> 19.2 us
    unnamed x12 -> x19, local copies, waits for them, and re-layouts: 0.03 us -> 4.55 us
where the time goes in v1:
time: 149 us; the launch traced here: 148 us
  waiting for transfers between devices  41.1 us (28%)
  matrix products  40.1 us (27%)
  local copies, waits for them, and re-layouts  19.2 us (13%)
  other arithmetic  16 us (11%)
  between operations  13.6 us (9%)
  blocking collectives  10.4 us (7%)
  starting transfers between devices  7.5 us (5%)
    reduce_scatter x1, waiting for transfers between devices, local(): lax.psum_scatter(partial_sums, 'hidden', scatter_dimension=0, tiled=True)  26.9 us
    dot_general x1, matrix products, local(): jnp.einsum('ntf,tfd->ntd', activated, w_down, preferred_element_type=jnp....  17.5 us
    all_to_all x1, waiting for transfers between devices, track_blocks(): jax.lax.all_to_all(a_next, concat_axis=0, split_axis=0, axis_name='token')  14.2 us
    all_gather x1, blocking collectives, local(): lax.all_gather(normed, 'hidden', axis=0, tiled=True)  10.4 us
    dot_general x1, matrix products, combine_blocks(): jnp.einsum('nr,nqhs->rqhs', owned, factor[..., None] * weighted, precisio...  8.84 us
    convert_element_type x6, local copies, waits for them, and re-layouts, local(): joined = mixed_rows.astype(jnp.float32) + unmixed.astype(jnp.float32)  8.46 us
    all_to_all x1, starting transfers between devices, track_blocks(): jax.lax.all_to_all(a_next, concat_axis=0, split_axis=0, axis_name='token')  7.28 us
    dot_general x1, matrix products, block_partials(): jnp.einsum('qhs,nhsp->nqhp', query_heads, slot_keys, preferred_element_ty...  6.72 us
  transfers between devices with their start and end apart: 2, of which 2 were waited for; matrix products, arithmetic and copies ran while one was open for 0% of the time, Pallas kernels for 0%

profile of v1, /device:TPU:0, one launch (start us, length us, event | category | flops | bytes accessed | tf_op | source)
XLA Modules:
  0.0 147.9 jit_solution(4233486902186870317)
XLA Ops:
  6.5 0.7 reshape.208
  8.5 0.8 reshape.211
  9.3 6.7 %bitcast_reduce_fusion = (f32[96,32,4]{1,0,2:T(8,128)S(1)}, f32[4,96,128,32]{2,3,1,0:T(8,128)}) fusion(pred[96,128]{1,0:T(8,128)(4,1)S(1)} %iota_compare_fusion, bf16[96,4,48,128]{3,2,1,0:T(8,128)(2,1)} %bitcast.159, bf16[32,4,48,1]{2,1,0,3:T(4,128)(2,1)S(1)} %bitcast.161), kind=kOutput, calls=%fused_computation.2 | convolution fusion | flops 155701248 | bytes 11083776 | tf_op jit(solution)/shard_map/qhs,nhsp->nqhp/dot_general | solution.py:30
  16.1 0.7 copy.68
  16.8 6.0 %fusion.6 = (f32[96,32,4]{1,0,2:T(8,128)S(1)}, bf16[96,32,4,128]{3,1,0,2:T(8,128)(2,1)S(1)}) fusion(f32[4,96,128,32]{2,3,1,0:T(8,128)} %get-tuple-element.12, f32[96,32,4]{1,0,2:T(8,128)S(1)} %get-tuple-element.11, pred[96,128]{1,0:T(8,128)(4,1)S(1)} %iota_compare_fusion), kind=kLoop, calls=%fused_computation.10 | loop fusion | flops 9424896 | bytes 9547776 | tf_op jit(solution)/shard_map/reduce_sum | solution.py:38
  22.8 0.7 copy.72
  23.5 1.5 select_reduce_fusion
  25.0 1.1 fusion.32
  26.2 1.1 fusion.76
  27.4 4.8 %bitcast_multiply_fusion = f32[96,32,4,48]{3,1,2,0:T(8,128)S(1)} fusion(f32[96,32,4]{1,2,0:T(4,128)S(1)} %copy.69, bf16[96,4,48,128]{3,2,1,0:T(8,128)(2,1)} %bitcast.158, bf16[96,32,4,128]{3,1,0,2:T(8,128)(2,1)S(1)} %get-tuple-element.10), kind=kOutput, calls=%fused_computation | convolution fusion | flops 151584768 | bytes 10272768 | tf_op jit(solution)/shard_map/nqhp,nhsp->nqhs/dot_general | solution.py:39
  32.3 8.8 %divide_convert_fusion = (bf16[32,32,4,48]{3,0,2,1:T(8,128)(2,1)S(1)}, f32[32,32,4,48]{3,0,2,1:T(8,128)}) fusion(f32[32,32,4]{0,2,1:T(4,128)S(1)} %copy.75, f32[96,32,4,48]{3,1,2,0:T(8,128)S(1)} %bitcast_multiply_fusion, s32[96]{0:T(128)S(1)} %copy-done.3), kind=kOutput, calls=%fused_computation.20 | convolution fusion | flops 226888704 | bytes 3555712 | tf_op jit(solution)/shard_map/nr,nqhs->rqhs/dot_general | solution.py:56
  42.2 0.6 fusion.74
  42.9 0.7 fusion.73
  43.5 0.6 fusion.72
  44.2 0.7 fusion.71
  44.8 0.6 fusion.70
  45.5 0.7 fusion.69
  46.1 0.6 fusion.68
  46.8 0.7 fusion.67
  47.4 7.3 %all-to-all-start = ((bf16[8,32,4,192]{3,2,1,0:T(4,128)(2,1)}), bf16[8,32,4,192]{3,2,1,0:T(4,128)(2,1)S(1)}, u32[]{:S(2)}, u32[]{:S(2)}) async-start(bf16[8,32,4,192]{3,2,1,0:T(4,128)(2,1)} %fusion.67), calls=%async_computation | async-start | bytes 1048576 | tf_op jit(solution)/shard_map/all_to_all | solution.py:92
  55.0 14.2 %all-to-all-done = bf16[8,32,4,192]{3,2,1,0:T(4,128)(2,1)S(1)} async-done(((bf16[8,32,4,192]{3,2,1,0:T(4,128)(2,1)}), bf16[8,32,4,192]{3,2,1,0:T(4,128)(2,1)S(1)}, u32[]{:S(2)}, u32[]{:S(2)}) %all-to-all-start) | async-done | bytes 393248 | tf_op jit(solution)/shard_map/all_to_all | solution.py:92
  69.9 0.6 copy.79
  70.6 1.3 reshape.215
  72.3 3.9 %fusion.34 = (f32[32,4]{0,1:T(4,128)S(1)}, f32[32,4,32,48]{3,0,1,2:T(8,128)S(1)}) fusion(f32[32,4,32,48]{3,2,1,0:T(8,128)S(1)} %reshape.216, f32[32,4,32]{0,1,2:T(4,128)S(1)} %copy.73, f32[32,32,4,48]{3,0,2,1:T(8,128)} %get-tuple-element.14), kind=kLoop, calls=%fused_computation.50 | loop fusion | flops 982912 | bytes 2376192 | tf_op jit(solution)/shard_map/reduce_sum | solution.py:63
  76.2 2.6 %copy.74 = f32[32,4,32,48]{3,2,0,1:T(8,128)} copy(f32[32,4,32,48]{3,0,1,2:T(8,128)S(1)} %get-tuple-element.8) | data formatting | bytes 1572864 | tf_op jit(solution)/shard_map/convert_element_type | solution.py:99
  78.8 1.4 multiply_reduce_fusion
  80.2 2.9 %reshape.214 = f32[32,4,1536]{2,0,1:T(8,128)S(1)} reshape(f32[32,4,32,48]{3,2,0,1:T(8,128)} %copy.74) | data formatting | bytes 1572864 | tf_op jit(solution)/shard_map/convert_element_type | solution.py:99
  83.4 10.4 %all_gather.3 = bf16[64,4,1536]{2,0,1:T(8,128)(2,1)S(1)} all-gather(bf16[32,4,1536]{2,0,1:T(8,128)(2,1)S(1)} %multiply_convert_fusion.1), channel_id=1, replica_groups=mesh['batch'=2,'token'=8,'hidden'=2] {'hidden'}, dimensions={0}, use_global_device_ids=true | all-gather | bytes 1179648 | tf_op jit(solution)/shard_map/all_gather | solution.py:103
  93.8 17.5 %convolution_bitcast_fusion = f32[64,4,1536]{2,0,1:T(8,128)} fusion(bf16[4,1536,1536]{2,1,0:T(8,128)(2,1)} %param.14, bf16[64,4,1536]{2,0,1:T(8,128)(2,1)S(1)} %all_gather.3, bf16[4,1536,1536]{2,1,0:T(8,128)(2,1)} %param.13), kind=kOutput, calls=%fused_computation.14 | convolution fusion | flops 2441478144 | bytes 40108032 | tf_op jit(solution)/shard_map/ntf,tfd->ntd/dot_general | solution.py:108
  111.3 26.9 %reduce-scatter.2.cloned.1.call-done = f32[32,4,1536]{2,0,1:T(8,128)} async-done(((f32[64,4,1536]{2,0,1:T(8,128)}), f32[32,4,1536]{2,0,1:T(8,128)}) %reduce-scatter.2.cloned.1.call-update) | async-done | bytes 786448 | tf_op jit(solution)/shard_map/reduce_scatter | solution.py:109
  138.2 1.4 fusion.66
  140.0 1.1 copy.82
  (43 shorter events, 4.8 us)
Async XLA Ops:
  7.7 0.7 copy-start.2
  27.4 4.9 %copy-start.3 = (s32[96]{0:T(128)S(1)}, s32[96]{0:T(128)}, u32[]{:S(2)}) copy-start(s32[96]{0:T(128)} %copy-done.2) | copy-start | bytes 1156
  47.4 21.8 %all-to-all-start = ((bf16[8,32,4,192]{3,2,1,0:T(4,128)(2,1)}), bf16[8,32,4,192]{3,2,1,0:T(4,128)(2,1)S(1)}, u32[]{:S(2)}, u32[]{:S(2)}) async-start(bf16[8,32,4,192]{3,2,1,0:T(4,128)(2,1)} %fusion.67), calls=%async_computation | async-start | bytes 1048576 | tf_op jit(solution)/shard_map/all_to_all | solution.py:92
  54.7 83.5 %reduce-scatter.2.cloned.1.call-start = ((), (), s32[]{:S(2)}) async-start(), calls=%async_computation.2 | async-start | bytes 2359296 | tf_op jit(solution)/shard_map/reduce_scatter | solution.py:109
  80.2 2.9 %copy-start.1 = (f32[32,4,1536]{2,0,1:T(8,128)S(1)}, f32[32,4,1536]{2,0,1:T(8,128)}, u32[]{:S(2)}) copy-start(f32[32,4,1536]{2,0,1:T(8,128)} %reshape.215) | copy-start | bytes 2359300
  80.2 2.9 %copy-start.4 = (f32[1536]{0:T(1024)S(1)}, f32[1536]{0:T(1024)}, u32[]{:S(2)}) copy-start(f32[1536]{0:T(1024)} %param.12) | copy-start | bytes 18436
  111.3 28.5 %copy-start.5 = (f32[1536]{0:T(1024)S(1)}, f32[1536]{0:T(1024)}, u32[]{:S(2)}) copy-start(f32[1536]{0:T(1024)} %param.15) | copy-start | bytes 18436
  138.2 1.4 copy-start
Sparse Core Ops, SparseCore 0:
  111.4 26.7 reduce-scatter.1
